TPU v7x, 16 devices: a 4x2x1 block of a 4x4x8 slice. The times are simulated.
16 devices in a mesh: dp: 2 (over y, z), wg: 8 (over x, core).
Axes of the slice: x: 4, y: 2, z: 1, core: 2. Of those that a mesh axis runs over, the one named last changes fastest.
The devices are a block of a 4x4x8 slice.
Arguments:
- hidden: bfloat16 [65536, 1024], P(('dp', 'wg')), parts along dimension 0
- choice: int32 [65536, 8], P(('dp', 'wg')), parts along dimension 0
- pre_scale: float32 [1024], replicated
- w_router: bfloat16 [1024, 32], replicated
- w_gelu: bfloat16 [32, 1024, 512], P(None, None, 'wg')
- w_linear: bfloat16 [32, 1024, 512], P(None, None, 'wg')
- w_down: bfloat16 [32, 512, 1024], P(None, 'wg')
- post_scale: float32 [1024], replicated
Outputs:
- output: bfloat16 [65536, 1024], P(('dp', 'wg')), parts along dimension 0
There are 2 independent parts. A program takes and returns all parts, laid end to end along the dimension named above; an argument that names none is the same for every part.
All inputs are finite; a program needn't handle non-finite values.
Results may differ from a plain program's by a relative error of at most 0.001.
Values are sent between devices in bfloat16 or wider.
A program may use at most 768 MiB of HBM per device.

v0:
```python
import jax
import jax.numpy as jnp
from jax import lax
from jax.sharding import PartitionSpec as P

EPS = 1e-5


def rms_norm(values, gain_vec):
    return values * lax.rsqrt(jnp.mean(values * values, axis=-1, keepdims=True) + EPS) * gain_vec


def route_slots(block_ids, num_experts, capacity):
    tok_rows, top_k = block_ids.shape
    flat_ids = block_ids.reshape(-1)
    sort_order = jnp.argsort(flat_ids, stable=True)
    counts = jnp.sum((flat_ids[:, None] == jnp.arange(num_experts)[None, :]).astype(jnp.int32), axis=0)
    starts = jnp.cumsum(counts) - counts
    slot_rank = jnp.arange(capacity)
    source = jnp.minimum(starts[:, None] + slot_rank[None, :], tok_rows * top_k - 1)
    slot_token = sort_order[source].reshape(-1) // top_k
    sorted_pos = jnp.argsort(sort_order, stable=True)
    slot_of = flat_ids * capacity + sorted_pos - starts[flat_ids]
    return slot_token, slot_of


def solution(mesh):
    def local_block(hidden, choice, pre_scale, w_router, w_gelu, w_linear, w_down, post_scale):
        tok_rows, d_model = hidden.shape
        num_experts = w_gelu.shape[0]
        top_k = choice.shape[1]
        capacity = 2 * tok_rows * top_k // num_experts
        hidden_f = hidden.astype(jnp.float32)
        normed = rms_norm(hidden_f, pre_scale).astype(jnp.bfloat16)
        router_probs = jax.nn.softmax(jnp.dot(normed, w_router, preferred_element_type=jnp.float32), axis=-1)
        gate_vals = jnp.take_along_axis(router_probs, choice, axis=1)
        slot_token, slot_of = route_slots(choice, num_experts, capacity)
        dispatched = jnp.take(normed, slot_token, axis=0).reshape(num_experts, capacity, d_model)

        def one_expert(expert_args):
            expert_rows, gelu_part, linear_part, down_part = expert_args
            gelu_full = lax.all_gather(gelu_part, 'wg', axis=1, tiled=True)
            linear_full = lax.all_gather(linear_part, 'wg', axis=1, tiled=True)
            down_full = lax.all_gather(down_part, 'wg', axis=0, tiled=True)
            gelu_in = jnp.dot(expert_rows, gelu_full, preferred_element_type=jnp.float32)
            linear_in = jnp.dot(expert_rows, linear_full, preferred_element_type=jnp.float32)
            hidden_act = (jax.nn.gelu(gelu_in, approximate=True) * linear_in).astype(jnp.bfloat16)
            return jnp.dot(hidden_act, down_full, preferred_element_type=jnp.float32)

        expert_out = lax.map(one_expert, (dispatched, w_gelu, w_linear, w_down)).reshape(num_experts * capacity, d_model)
        picked = jnp.take(expert_out, slot_of, axis=0).reshape(tok_rows, top_k, d_model)
        mixed_out = jnp.sum(picked * gate_vals[:, :, None], axis=1)
        return (hidden_f + rms_norm(mixed_out, post_scale)).astype(jnp.bfloat16)

    row_spec = P(('dp', 'wg'), None)
    weight_in = P(None, None, 'wg')
    return jax.shard_map(local_block, mesh=mesh, in_specs=(row_spec, row_spec, P(), P(), weight_in, weight_in, P(None, 'wg', None), P()), out_specs=row_spec, check_vma=False)
```

profile of v0, /device:TPU:113, one launch (start us, length us, event | category | flops | bytes accessed | tf_op | source)
XLA Modules:
  0.0 4235.6 jit_solution(782888848936060016)
XLA Ops:
  36.6 21.2 sort.32
  58.1 362.7 %gather_fusion = s32[65536]{0:T(1024)S(1)} fusion(s32[32768]{0:T(1024)S(1)} %get-tuple-element.39, s32[65536]{0:T(1024)S(1)} %broadcast_clamp_fusion.1), kind=kCustom, calls=%fused_computation | custom fusion | bytes 786432 | tf_op jit(solution)/shard_map/gather | solution.py:21
  462.9 260.6 %gather_fusion.3 = f32[32768]{0:T(1024)S(1)} fusion(f32[4096,32]{0,1:T(8,128)S(1)} %fusion.36, s32[32768]{0:T(1024)S(1)} %reshape.307), kind=kCustom, calls=%fused_computation.3 | custom fusion | bytes 524288 | tf_op jit(solution)/shard_map/jit(take_along_axis)/gather | solution.py:36
  727.2 321.8 %gather_fusion.1 = bf16[65536,1024]{1,0:T(8,128)(2,1)} fusion(bf16[4096,1024]{1,0:T(8,128)(2,1)} %copy-done.2, s32[65536]{0:T(1024)S(1)} %copy-done.6), kind=kCustom, calls=%fused_computation.1 | custom fusion | bytes 268697600 | tf_op jit(solution)/shard_map/jit(_take)/gather | solution.py:38
  1049.0 87.8 %broadcast_select_fusion = bf16[32,2048,1024]{2,1,0:T(8,128)(2,1)} fusion(bf16[32,2048,1024]{2,1,0:T(8,128)(2,1)} %bitcast.41, pred[32,2048]{1,0:T(8,128)(4,1)S(1)} %copy-done.8), kind=kLoop, calls=%fused_computation.36 | loop fusion | flops 67108864 | bytes 268500992 | tf_op jit(solution)/shard_map/jit(_take)/select_n | solution.py:38
  1136.7 2387.5 %while.10 = (s32[]{:T(128)}, f32[32,2048,1024]{2,1,0:T(8,128)}, bf16[32,2048,1024]{2,1,0:T(8,128)(2,1)}, bf16[32,1024,64]{1,2,0:T(8,128)(2,1)}, bf16[32,1024,64]...) while((s32[]{:T(128)}, f32[32,2048,1024]{2,1,0:T(8,128)}, bf16[32,2048,1024]{2,1,0:T(8,128)(2,1)}, ...), condition=%wide.region_6.7_spmd, body=%wide.region_5.6_spmd.sunk | while | flops 6452936704 | bytes 39716060 | solution.py:50
  1182.0 20.5 all-gather.17.cloned.1.call-done
  1331.0 20.5 all-gather.17.cloned.1.call-done
  1554.0 20.3 all-gather.17.cloned.1.call-done
  1628.5 20.5 all-gather.17.cloned.1.call-done
  1703.3 20.3 all-gather.17.cloned.1.call-done
  2150.7 20.5 all-gather.17.cloned.1.call-done
  2448.2 20.5 all-gather.17.cloned.1.call-done
  2522.9 20.5 all-gather.17.cloned.1.call-done
  2597.3 20.5 all-gather.17.cloned.1.call-done
  2746.3 20.3 all-gather.17.cloned.1.call-done
  2820.6 20.5 all-gather.17.cloned.1.call-done
  2969.3 20.5 all-gather.17.cloned.1.call-done
  3043.7 20.5 all-gather.17.cloned.1.call-done
  3118.5 20.5 all-gather.17.cloned.1.call-done
  3342.0 20.5 all-gather.17.cloned.1.call-done
  3491.2 20.5 all-gather.17.cloned.1.call-done
  3524.2 612.8 %gather_fusion.2 = f32[32768,1024]{1,0:T(8,128)} fusion(f32[65536,1024]{1,0:T(8,128)} %bitcast.42, s32[32768]{0:T(1024)S(1)} %copy-done.7), kind=kCustom, calls=%fused_computation.2 | custom fusion | bytes 268566528 | tf_op jit(solution)/shard_map/jit(_take)/gather | solution.py:51
  4137.0 72.8 %fusion.31 = f32[4096,1024]{1,0:T(8,128)} fusion(f32[32768,1024]{1,0:T(8,128)} %gather_fusion.2, f32[4096,8]{1,0:T(8,128)S(1)} %copy-done.3, pred[4096,8]{1,0:T(8,128)(4,1)S(1)} %copy-done.4), kind=kLoop, calls=%fused_computation.35 | loop fusion | flops 96468992 | bytes 151158784 | tf_op jit(solution)/shard_map/reduce_sum | solution.py:52
  (496 shorter events, 2153.5 us)
Async XLA Ops:
  1140.2 62.3 %all-gather.17.cloned.1.call-start = ((), (), s32[]{:S(2)}) async-start(), calls=%async_computation.2 | async-start | bytes 1179648 | tf_op jit(solution)/shard_map/while/body/eval_jaxpr/all_gather | solution.py:42
  1292.5 58.9 %all-gather.17.cloned.1.call-start = ((), (), s32[]{:S(2)}) async-start(), calls=%async_computation.2 | async-start | bytes 1179648 | tf_op jit(solution)/shard_map/while/body/eval_jaxpr/all_gather | solution.py:42
  1367.3 58.5 %all-gather.17.cloned.1.call-start = ((), (), s32[]{:S(2)}) async-start(), calls=%async_computation.2 | async-start | bytes 1179648 | tf_op jit(solution)/shard_map/while/body/eval_jaxpr/all_gather | solution.py:42
  1441.6 58.6 %all-gather.17.cloned.1.call-start = ((), (), s32[]{:S(2)}) async-start(), calls=%async_computation.2 | async-start | bytes 1179648 | tf_op jit(solution)/shard_map/while/body/eval_jaxpr/all_gather | solution.py:42
  1590.2 58.8 %all-gather.17.cloned.1.call-start = ((), (), s32[]{:S(2)}) async-start(), calls=%async_computation.2 | async-start | bytes 1179648 | tf_op jit(solution)/shard_map/while/body/eval_jaxpr/all_gather | solution.py:42
  1664.8 58.8 %all-gather.17.cloned.1.call-start = ((), (), s32[]{:S(2)}) async-start(), calls=%async_computation.2 | async-start | bytes 1179648 | tf_op jit(solution)/shard_map/while/body/eval_jaxpr/all_gather | solution.py:42
  1739.5 58.6 %all-gather.17.cloned.1.call-start = ((), (), s32[]{:S(2)}) async-start(), calls=%async_computation.2 | async-start | bytes 1179648 | tf_op jit(solution)/shard_map/while/body/eval_jaxpr/all_gather | solution.py:42
  1813.9 58.8 %all-gather.17.cloned.1.call-start = ((), (), s32[]{:S(2)}) async-start(), calls=%async_computation.2 | async-start | bytes 1179648 | tf_op jit(solution)/shard_map/while/body/eval_jaxpr/all_gather | solution.py:42
  1888.6 58.8 %all-gather.17.cloned.1.call-start = ((), (), s32[]{:S(2)}) async-start(), calls=%async_computation.2 | async-start | bytes 1179648 | tf_op jit(solution)/shard_map/while/body/eval_jaxpr/all_gather | solution.py:42
  1963.2 58.8 %all-gather.17.cloned.1.call-start = ((), (), s32[]{:S(2)}) async-start(), calls=%async_computation.2 | async-start | bytes 1179648 | tf_op jit(solution)/shard_map/while/body/eval_jaxpr/all_gather | solution.py:42
  2112.3 58.9 %all-gather.17.cloned.1.call-start = ((), (), s32[]{:S(2)}) async-start(), calls=%async_computation.2 | async-start | bytes 1179648 | tf_op jit(solution)/shard_map/while/body/eval_jaxpr/all_gather | solution.py:42
  2409.9 58.8 %all-gather.17.cloned.1.call-start = ((), (), s32[]{:S(2)}) async-start(), calls=%async_computation.2 | async-start | bytes 1179648 | tf_op jit(solution)/shard_map/while/body/eval_jaxpr/all_gather | solution.py:42
  2484.5 58.9 %all-gather.17.cloned.1.call-start = ((), (), s32[]{:S(2)}) async-start(), calls=%async_computation.2 | async-start | bytes 1179648 | tf_op jit(solution)/shard_map/while/body/eval_jaxpr/all_gather | solution.py:42
  2559.3 58.5 %all-gather.17.cloned.1.call-start = ((), (), s32[]{:S(2)}) async-start(), calls=%async_computation.2 | async-start | bytes 1179648 | tf_op jit(solution)/shard_map/while/body/eval_jaxpr/all_gather | solution.py:42
  2633.6 58.8 %all-gather.17.cloned.1.call-start = ((), (), s32[]{:S(2)}) async-start(), calls=%async_computation.2 | async-start | bytes 1179648 | tf_op jit(solution)/shard_map/while/body/eval_jaxpr/all_gather | solution.py:42
  2782.5 58.6 %all-gather.17.cloned.1.call-start = ((), (), s32[]{:S(2)}) async-start(), calls=%async_computation.2 | async-start | bytes 1179648 | tf_op jit(solution)/shard_map/while/body/eval_jaxpr/all_gather | solution.py:42
  2857.0 58.5 %all-gather.17.cloned.1.call-start = ((), (), s32[]{:S(2)}) async-start(), calls=%async_computation.2 | async-start | bytes 1179648 | tf_op jit(solution)/shard_map/while/body/eval_jaxpr/all_gather | solution.py:42
  3005.6 58.6 %all-gather.17.cloned.1.call-start = ((), (), s32[]{:S(2)}) async-start(), calls=%async_computation.2 | async-start | bytes 1179648 | tf_op jit(solution)/shard_map/while/body/eval_jaxpr/all_gather | solution.py:42
  3080.1 58.9 %all-gather.17.cloned.1.call-start = ((), (), s32[]{:S(2)}) async-start(), calls=%async_computation.2 | async-start | bytes 1179648 | tf_op jit(solution)/shard_map/while/body/eval_jaxpr/all_gather | solution.py:42
  3154.9 58.5 %all-gather.17.cloned.1.call-start = ((), (), s32[]{:S(2)}) async-start(), calls=%async_computation.2 | async-start | bytes 1179648 | tf_op jit(solution)/shard_map/while/body/eval_jaxpr/all_gather | solution.py:42
  3229.3 58.6 %all-gather.17.cloned.1.call-start = ((), (), s32[]{:S(2)}) async-start(), calls=%async_computation.2 | async-start | bytes 1179648 | tf_op jit(solution)/shard_map/while/body/eval_jaxpr/all_gather | solution.py:42
  3303.8 58.6 %all-gather.17.cloned.1.call-start = ((), (), s32[]{:S(2)}) async-start(), calls=%async_computation.2 | async-start | bytes 1179648 | tf_op jit(solution)/shard_map/while/body/eval_jaxpr/all_gather | solution.py:42
  3378.3 58.6 %all-gather.17.cloned.1.call-start = ((), (), s32[]{:S(2)}) async-start(), calls=%async_computation.2 | async-start | bytes 1179648 | tf_op jit(solution)/shard_map/while/body/eval_jaxpr/all_gather | solution.py:42
  3452.8 58.9 %all-gather.17.cloned.1.call-start = ((), (), s32[]{:S(2)}) async-start(), calls=%async_computation.2 | async-start | bytes 1179648 | tf_op jit(solution)/shard_map/while/body/eval_jaxpr/all_gather | solution.py:42
  (83 other events, 7760.7 us)
Sparse Core Ops, SparseCore 0:
  1139.2 22.2 all-gather.12
  1163.1 18.8 all-gather.14
  1183.6 18.8 all-gather.16
  1312.1 18.8 all-gather.14
  1332.6 18.8 all-gather.16
  1366.1 18.8 all-gather.12
  1514.8 18.8 all-gather.12
  1630.1 18.8 all-gather.16
  1684.4 18.8 all-gather.14
  1833.5 18.8 all-gather.14
  1908.2 18.8 all-gather.14
  1982.7 18.8 all-gather.14
  2003.1 18.8 all-gather.16
  2131.8 18.8 all-gather.14
  2152.3 18.8 all-gather.16
  2449.8 18.8 all-gather.16
  2504.1 18.8 all-gather.14
  2524.6 18.8 all-gather.16
  2747.8 18.8 all-gather.16
  2970.9 18.8 all-gather.16
  3099.7 18.8 all-gather.14
  3120.2 18.8 all-gather.16
  3472.4 18.8 all-gather.14
  3492.8 18.8 all-gather.16
  (72 shorter events, 1352.3 us)
where the time goes:
time: 4260 us; the launch traced here: 4240 us
  local copies, waits for them, and re-layouts  1720 us (40%)
  waiting for transfers between devices  1610 us (38%)
  matrix products  624 us (15%)
  other arithmetic  261 us (6%)
    all_gather x32, waiting for transfers between devices, one_expert(): gelu_full = lax.all_gather(gelu_part, 'wg', axis=1, tiled=True)  653 us
    gather x1, local copies, waits for them, and re-layouts, local_block(): jnp.take(expert_out, slot_of, axis=0).reshape(tok_rows, top_k, d_model)  613 us
    all_gather x32, waiting for transfers between devices, one_expert(): linear_full = lax.all_gather(linear_part, 'wg', axis=1, tiled=True)  519 us
    all_gather x32, waiting for transfers between devices, one_expert(): down_full = lax.all_gather(down_part, 'wg', axis=0, tiled=True)  434 us
    dot_general x32, matrix products, one_expert(): return jnp.dot(hidden_act, down_full, preferred_element_type=jnp.float32)  401 us
    gather x2, local copies, waits for them, and re-layouts, route_slots(): slot_token = sort_order[source].reshape(-1) // top_k  363 us
    gather x1, local copies, waits for them, and re-layouts, local_block(): jnp.take(normed, slot_token, axis=0).reshape(num_experts, capacity, d_model)  322 us
    gather x5, local copies, waits for them, and re-layouts, local_block(): gate_vals = jnp.take_along_axis(router_probs, choice, axis=1)  264 us
  transfers between devices with their start and end apart: 96, of which 96 were waited for; matrix products, arithmetic and copies ran while one was open for 8% of the time, Pallas kernels for 0%

commit v1 on v0

v1 whole, which is shorter than its diff:
```python
import functools

import jax
import jax.numpy as jnp
from jax import lax
from jax.experimental import pallas as pl
from jax.experimental.pallas import tpu as pltpu
from jax.sharding import PartitionSpec as P

EPS = 1e-5
LANES = 128
SUB = 8
TILE = 256
PRE_TILE = 1024
PRE_PART = 256
POST_TILE = 256
GROUP = 8
CHUNKS = (4, 6, 6, 6, 4, 3, 2, 1)
VMEM_LIMIT = 64 * 1024 * 1024 - 65536
NT = (((1,), (1,)), ((), ()))


def gate_pitch(t_rows):
    return t_rows + SUB * LANES


def pre_kernel(h_ref, gain_ref, wr_ref, x_ref, p_ref):
    rows, d_model = h_ref.shape
    for r0 in range(0, rows, PRE_PART):
        h = h_ref[r0:r0 + PRE_PART, :].astype(jnp.float32)
        scale = lax.rsqrt(jnp.mean(h * h, axis=-1, keepdims=True) + EPS)
        b = (h * scale * gain_ref[...]).astype(jnp.bfloat16)
        logits = lax.dot_general(wr_ref[...], b, NT, preferred_element_type=jnp.float32)
        peak = jnp.max(logits, axis=0, keepdims=True)
        e = jnp.exp(logits - peak)
        probs = e / jnp.sum(e, axis=0, keepdims=True)
        for j in range(PRE_PART // LANES):
            p_ref[:, r0 // LANES + j, :] = probs[:, j * LANES:(j + 1) * LANES]
        bf = b.astype(jnp.float32)
        for j in range(d_model // LANES):
            x_ref[pl.ds(r0 * SUB + j, PRE_PART, stride=SUB), :] = bf[:, j * LANES:(j + 1) * LANES]


def moe_kernel(first, last, e0, *refs):
    list_hbm, tstart_ref, gate_hbm, x_hbm, w_hbm = refs[:5]
    refs = refs[5:]
    if not first:
        y_in, refs = refs[0], refs[1:]
    if last:
        hid_hbm, post_ref, refs = refs[0], refs[1], refs[2:]
    y_out, refs = refs[0], refs[1:]
    list_ref, gate_ref, x_v, y_v, wg_v, wl_v, wd_v, xs, os_, xb, ab, wsem, xsem, ysem, lsem, gsem = refs[:16]
    if last:
        hbuf, obuf, hsem, osem = refs[16:]

    shards, _, e_c, f_dev, d_model = w_hbm.shape
    t_rows = x_hbm.shape[0] // SUB
    dff = shards * f_dev
    nj = d_model // LANES
    pitch = TILE + 1
    half = dff // 2

    def w_copies(e, slot):
        return [
            pltpu.make_async_copy(w_hbm.at[:, k, e], buf.at[slot], wsem.at[slot, k])
            for k, buf in enumerate((wg_v, wl_v, wd_v))
        ]

    t_begin = tstart_ref[e0]
    t_end = tstart_ref[e0 + e_c]
    span = list_ref.shape[0] // TILE
    tiles = list_hbm.shape[0] // TILE
    align = max(1, SUB * LANES // TILE)
    l_first = jnp.minimum(t_begin // align * align, tiles - span)
    l_copy = pltpu.make_async_copy(list_hbm.at[pl.ds(pl.multiple_of(l_first * TILE, align * TILE), span * TILE)], list_ref, lsem)
    g_copy = pltpu.make_async_copy(gate_hbm.at[pl.ds(e0 * gate_pitch(t_rows), e_c * gate_pitch(t_rows))], gate_ref, gsem)
    l_copy.start()
    g_copy.start()
    x_copy = pltpu.make_async_copy(x_hbm, x_v.at[pl.ds(0, t_rows * SUB)], xsem)
    x_copy.start()
    for c in w_copies(0, 0):
        c.start()
    if not first:
        y_copy = pltpu.make_async_copy(y_in, y_v, ysem)
        y_copy.start()
    else:
        def zero(i, _):
            y_v[pl.ds(pl.multiple_of(i * 64, 64), 64), :] = jnp.zeros((64, LANES), jnp.float32)
            return 0
        lax.fori_loop(0, y_v.shape[0] // 64, zero, 0)
    x_v[pl.ds(t_rows * SUB, SUB), :] = jnp.zeros((SUB, LANES), jnp.float32)
    l_copy.wait()
    g_copy.wait()
    x_copy.wait()

    def gather(tile):
        base = jnp.minimum(tile - l_first, span - 1) * TILE
        for m in range(TILE):
            t = list_ref[base + m]
            xs[pl.ds(m, SUB, stride=pitch), :] = x_v[pl.ds(pl.multiple_of(t * SUB, SUB), SUB), :]

    def combine(tile, e):
        base = (tile - l_first) * TILE
        gbase = e * gate_pitch(t_rows)
        for m0 in range(0, TILE, GROUP):
            toks, vals = [], []
            for m in range(m0, m0 + GROUP):
                t = list_ref[base + m]
                g = gate_ref[gbase + t]
                row = pl.ds(pl.multiple_of(t * SUB, SUB), SUB)
                toks.append(row)
                vals.append(y_v[row, :] + g * os_[pl.ds(m, SUB, stride=pitch), :])
            for row, val in zip(toks, vals):
                y_v[row, :] = val

    def matmuls(slot):
        for h in range(2):
            sh = shards // 2
            wg = wg_v[slot, h * sh:(h + 1) * sh].reshape(half, d_model)
            wl = wl_v[slot, h * sh:(h + 1) * sh].reshape(half, d_model)
            uv = lax.dot_general(xb[...], jnp.concatenate([wg, wl], axis=0), NT, preferred_element_type=jnp.float32)
            u, v = uv[:, :half], uv[:, half:]
            ab[:, h * half:(h + 1) * half] = (jax.nn.gelu(u, approximate=True) * v).astype(jnp.bfloat16)
        wd = wd_v[slot].reshape(dff, d_model)
        for n in range(2):
            width = d_model // 2
            o = jnp.dot(ab[...], wd[:, n * width:(n + 1) * width], preferred_element_type=jnp.float32)
            for j in range(width // LANES):
                os_[pl.ds((n * width // LANES + j) * pitch, TILE), :] = o[:, j * LANES:(j + 1) * LANES]

    def enter(e):
        slot = lax.rem(e, 2)
        for c in w_copies(e, slot):
            c.wait()

        @pl.when(e + 1 < e_c)
        def _():
            for c in w_copies(e + 1, 1 - slot):
                c.start()

    gather(t_begin)
    for j in range(nj):
        os_[pl.ds(j * pitch, TILE), :] = jnp.zeros((TILE, LANES), jnp.float32)
    enter(jnp.int32(0))
    if not first:
        y_copy.wait()

    def body(tile, e_prev):
        new = tile >= tstart_ref[e0 + e_prev + 1]
        e = e_prev + new.astype(jnp.int32)

        @pl.when(new)
        def _():
            enter(e)

        for j in range(nj):
            xb[:, j * LANES:(j + 1) * LANES] = xs[pl.ds(j * pitch, TILE), :].astype(jnp.bfloat16)
        gather(tile + 1)
        combine(jnp.maximum(tile - 1, t_begin), e_prev)
        matmuls(lax.rem(e, 2))
        return e

    e_last = lax.fori_loop(t_begin, t_end, body, jnp.int32(0))
    combine(t_end - 1, e_last)

    if not last:
        out = pltpu.make_async_copy(y_v, y_out, ysem)
        out.start()
        out.wait()
        return

    n_post = t_rows // POST_TILE

    def h_copy(i, slot):
        return pltpu.make_async_copy(hid_hbm.at[pl.ds(pl.multiple_of(i * POST_TILE, POST_TILE), POST_TILE)], hbuf.at[slot], hsem.at[slot])

    def o_copy(i, slot):
        return pltpu.make_async_copy(obuf.at[slot], y_out.at[pl.ds(pl.multiple_of(i * POST_TILE, POST_TILE), POST_TILE)], osem.at[slot])

    h_copy(0, 0).start()

    def post(i, _):
        slot = lax.rem(i, 2)

        @pl.when(i + 1 < n_post)
        def _():
            h_copy(i + 1, 1 - slot).start()

        @pl.when(i >= 2)
        def _():
            o_copy(i - 2, slot).wait()

        h_copy(i, slot).wait()
        parts = [y_v[pl.ds(i * POST_TILE * SUB + j, POST_TILE, stride=SUB), :] for j in range(nj)]
        square = parts[0] * parts[0]
        for part in parts[1:]:
            square = square + part * part
        scale = lax.rsqrt(jnp.sum(square, axis=-1, keepdims=True) / d_model + EPS)
        for j in range(nj):
            cols = slice(j * LANES, (j + 1) * LANES)
            val = hbuf[slot, :, cols].astype(jnp.float32) + parts[j] * scale * post_ref[:, cols]
            obuf[slot, :, cols] = val.astype(jnp.bfloat16)
        o_copy(i, slot).start()
        return 0

    lax.fori_loop(0, n_post, post, 0)
    for i in range(max(0, n_post - 2), n_post):
        o_copy(i, i % 2).wait()


def run_pre(hidden, pre_scale, w_router, interpret=False):
    t_rows, d_model = hidden.shape
    num_experts = w_router.shape[1]
    return pl.pallas_call(
        pre_kernel,
        grid=(t_rows // PRE_TILE,),
        in_specs=[
            pl.BlockSpec((PRE_TILE, d_model), lambda i: (i, 0)),
            pl.BlockSpec((1, d_model), lambda i: (0, 0)),
            pl.BlockSpec((num_experts, d_model), lambda i: (0, 0)),
        ],
        out_specs=[
            pl.BlockSpec((PRE_TILE * SUB, LANES), lambda i: (i, 0)),
            pl.BlockSpec((num_experts, PRE_TILE // LANES, LANES), lambda i: (0, i, 0)),
        ],
        out_shape=[
            jax.ShapeDtypeStruct((t_rows * SUB, LANES), jnp.float32),
            jax.ShapeDtypeStruct((num_experts, gate_pitch(t_rows) // LANES, LANES), jnp.float32),
        ],
        name='pre',
        interpret=interpret,
    )(hidden, pre_scale.reshape(1, d_model), w_router.T)


def run_moe(first, last, e0, lists, tstart, gates, x, w, y, hidden, post_scale, interpret=False):
    shards, _, e_c, f_dev, d_model = w.shape
    t_rows = x.shape[0] // SUB
    align = max(1, SUB * LANES // TILE)
    span = min(lists.shape[0] // TILE, e_c * (t_rows // 2 // TILE) + align)
    y_rows = (t_rows + SUB) * SUB
    dff = shards * f_dev
    smem = pl.BlockSpec(memory_space=pltpu.SMEM)
    hbm = pl.BlockSpec(memory_space=pl.ANY)
    args = [lists, tstart, gates, x, w]
    specs = [hbm, smem, hbm, hbm, hbm]
    aliases = {}
    if not first:
        if not last:
            aliases = {len(args): 0}
        args.append(y)
        specs.append(hbm)
    scratch = [
        pltpu.SMEM((span * TILE,), jnp.int32),
        pltpu.SMEM((e_c * gate_pitch(t_rows),), jnp.float32),
        pltpu.VMEM((y_rows, LANES), jnp.float32),
        pltpu.VMEM((y_rows, LANES), jnp.float32),
        pltpu.VMEM((2, shards, f_dev, d_model), jnp.bfloat16),
        pltpu.VMEM((2, shards, f_dev, d_model), jnp.bfloat16),
        pltpu.VMEM((2, shards, f_dev, d_model), jnp.bfloat16),
        pltpu.VMEM((SUB * (TILE + 1), LANES), jnp.float32),
        pltpu.VMEM((SUB * (TILE + 1), LANES), jnp.float32),
        pltpu.VMEM((TILE, d_model), jnp.bfloat16),
        pltpu.VMEM((TILE, dff), jnp.bfloat16),
        pltpu.SemaphoreType.DMA((2, 3)),
        pltpu.SemaphoreType.DMA,
        pltpu.SemaphoreType.DMA,
        pltpu.SemaphoreType.DMA,
        pltpu.SemaphoreType.DMA,
    ]
    if last:
        args += [hidden, post_scale.reshape(1, d_model)]
        specs += [hbm, pl.BlockSpec(memory_space=pltpu.VMEM)]
        out_shape = jax.ShapeDtypeStruct((t_rows, d_model), jnp.bfloat16)
        scratch += [
            pltpu.VMEM((2, POST_TILE, d_model), jnp.bfloat16),
            pltpu.VMEM((2, POST_TILE, d_model), jnp.bfloat16),
            pltpu.SemaphoreType.DMA((2,)),
            pltpu.SemaphoreType.DMA((2,)),
        ]
    else:
        out_shape = jax.ShapeDtypeStruct((y_rows, LANES), jnp.float32)
    rows = e_c * 1024
    return pl.pallas_call(
        functools.partial(moe_kernel, first, last, e0),
        in_specs=specs,
        out_specs=hbm,
        out_shape=out_shape,
        scratch_shapes=scratch,
        input_output_aliases=aliases,
        compiler_params=pltpu.CompilerParams(vmem_limit_bytes=VMEM_LIMIT),
        cost_estimate=pl.CostEstimate(flops=rows * 6 * d_model * dff, bytes_accessed=3 * y_rows * LANES * 4 + w.size * 2, transcendentals=0),
        name=f'moe_{e0}',
        interpret=interpret,
    )(*args)


def make_lists(choice_t, num_experts):
    top_k, t_rows = choice_t.shape
    big = 2 * t_rows
    keys = choice_t * big + lax.broadcasted_iota(jnp.int32, choice_t.shape, 1)
    experts = lax.broadcasted_iota(jnp.int32, (num_experts, 1, 1), 0)
    counts = jnp.sum((choice_t[None] == experts).astype(jnp.int32), axis=(1, 2))
    tiles = (counts + TILE - 1) // TILE
    pad = tiles * TILE - counts
    slot = lax.broadcasted_iota(jnp.int32, (num_experts, TILE), 1)
    owner = lax.broadcasted_iota(jnp.int32, (num_experts, TILE), 0)
    fill = jnp.where(slot < pad[:, None], owner, num_experts) * big + t_rows
    ordered = lax.sort(jnp.concatenate([keys.reshape(-1), fill.reshape(-1)]), is_stable=False)
    lists = ordered & (big - 1)
    tstart = jnp.concatenate([jnp.zeros((1,), jnp.int32), jnp.cumsum(tiles)])
    return lists, tstart


def solution(mesh):
    def local_block(hidden, choice, pre_scale, w_router, w_gelu, w_linear, w_down, post_scale):
        t_rows, d_model = hidden.shape
        num_experts = w_gelu.shape[0]
        gelu_t = jnp.swapaxes(w_gelu, 1, 2)
        linear_t = jnp.swapaxes(w_linear, 1, 2)
        weights = []
        e0 = 0
        for e_c in CHUNKS:
            part = jnp.stack([gelu_t[e0:e0 + e_c], linear_t[e0:e0 + e_c], w_down[e0:e0 + e_c]], axis=0)
            weights.append(lax.all_gather(part, 'wg', axis=0, tiled=False))
            e0 += e_c
        x, p = run_pre(hidden, pre_scale, w_router)
        gates = p.reshape(-1)
        lists, tstart = make_lists(choice.T, num_experts)
        y = None
        e0 = 0
        for c, e_c in enumerate(CHUNKS):
            y = run_moe(c == 0, c == len(CHUNKS) - 1, e0, lists, tstart, gates, x, weights[c], y, hidden, post_scale)
            e0 += e_c
        return y

    row_spec = P(('dp', 'wg'), None)
    weight_in = P(None, None, 'wg')
    return jax.shard_map(local_block, mesh=mesh, in_specs=(row_spec, row_spec, P(), P(), weight_in, weight_in, P(None, 'wg', None), P()), out_specs=row_spec, check_vma=False)
```

time: 4260 us -> 592 us (0.14)
  local copies, waits for them, and re-layouts: 1720 us -> 17.3 us
  waiting for transfers between devices: 1610 us -> 167 us
  matrix products: 624 us -> 0 us
  Pallas kernels: 0 us -> 359 us
  other arithmetic: 261 us -> 24.6 us
    gather x11 -> x0, local copies, waits for them, and re-layouts: 1560 us -> none  [the longest x1 613 us: local_block(): jnp.take(expert_out, slot_of, axis=0).reshape(tok_rows, top_k, d_model)]
    all_gather x96 -> x8, waiting for transfers between devices: 1600 us -> 167 us  [local_block(): weights.append(lax.all_gather(part, 'wg', axis=0, tiled=False))]
    dot_general x65 -> x0, matrix products: 624 us -> none  [the longest x32 401 us: one_expert(): return jnp.dot(hidden_act, down_full, preferred_element_type=jnp.float32)]
    pallas_call x0 -> x9, Pallas kernels: none -> 359 us  [the longest x8 347 us: run_moe(): pl.pallas_call(functools.partial(moe_kernel, first, last, e0), in_specs=s...]
    dynamic_slice x96 -> x0, local copies, waits for them, and re-layouts: 151 us -> none  [local_block(): lax.map(one_expert, (dispatched, w_gelu, w_linear, w_down))]
    select_n x3 -> x1, other arithmetic: 89.2 us -> 0.01 us  [make_lists(): tiles = (counts + TILE - 1) // TILE]
    reduce_sum x5 -> x1, other arithmetic: 85.4 us -> 0.7 us  [make_lists(): counts = jnp.sum((choice_t[None] == experts).astype(jnp.int32), axis=(1, 2))]
  transfers between devices with their start and end apart: 96 -> 8, of which waited for: 96 -> 6; matrix products, arithmetic and copies ran while one was open for 8% -> 6% of each run, Pallas kernels for 0% -> 56%
where the time goes in v1:
time: 592 us; the launch traced here: 583 us
  Pallas kernels  359 us (61%)
  waiting for transfers between devices  167 us (28%)
  other arithmetic  24.6 us (4%)
  local copies, waits for them, and re-layouts  17.3 us (3%)
  between operations  13.8 us (2%)
    pallas_call x8, Pallas kernels, run_moe(): pl.pallas_call(functools.partial(moe_kernel, first, last, e0), in_specs=s...  347 us
    all_gather x8, waiting for transfers between devices, local_block(): weights.append(lax.all_gather(part, 'wg', axis=0, tiled=False))  167 us
    another operation x10, local copies, waits for them, and re-layouts, local_block(): jnp.stack([gelu_t[e0:e0 + e_c], linear_t[e0:e0 + e_c], w_down[e0:e0 + e_c...  16.3 us
    another operation x8, other arithmetic, local_block(): jnp.stack([gelu_t[e0:e0 + e_c], linear_t[e0:e0 + e_c], w_down[e0:e0 + e_c...  13.1 us
  transfers between devices with their start and end apart: 8, of which 6 were waited for; matrix products, arithmetic and copies ran while one was open for 6% of the time, Pallas kernels for 56%

profile of v1, /device:TPU:113, one launch (start us, length us, event | category | flops | bytes accessed | tf_op | source)
XLA Modules:
  0.0 582.7 jit_solution(17422299833645484655)
XLA Ops:
  6.6 2.1 slice_bitcast_fusion.13
  8.6 2.7 slice_bitcast_fusion.9
  12.8 2.1 slice_bitcast_fusion.6
  15.7 3.3 slice_bitcast_fusion
  19.0 1.7 pad_maximum_fusion.2
  20.8 3.1 pad_maximum_fusion.1
  24.0 1.7 pad_maximum_fusion
  25.8 2.4 pad_maximum_fusion.3
  39.0 9.2 %sort.7 = s32[40960]{0:T(1024)S(1)} sort(s32[40960]{0:T(1024)S(1)} %pad_add_fusion), dimensions={0}, to_apply=%region_1.2 | sort | flops 655360 | bytes 327680 | tf_op jit(solution)/shard_map/sort | solution.py:308
  49.7 11.8 %pre.1 = (f32[32768,128]{1,0:T(8,128)}, f32[32,40,128]{2,1,0:T(8,128)}) custom-call(bf16[4096,1024]{1,0:T(8,128)(2,1)} %refs_6_.1, f32[1,1024]{1,0:T(1,128)} %bitcast.104, bf16[32,1024]{1,0:T(8,128)(2,1)} %bitcast.103), custom_call_target="tpu_custom_call" | custom-call | tf_op jit(solution)/shard_map/pre/pallas_call | solution.py:214
  61.5 17.9 %all-gather.31.cloned.1.call-done = bf16[24,4,64,1024]{3,2,1,0:T(8,128)(2,1)} async-done(((bf16[3,4,64,1024]{3,2,1,0:T(8,128)(2,1)}), bf16[24,4,64,1024]{3,2,1,0:T(8,128)(2,1)}) %all-gather.31.cloned.1.call-update) | async-done | bytes 12582928 | tf_op jit(solution)/shard_map/all_gather | solution.py:324
  79.4 37.0 %moe_0.1.refs_5_ = f32[32832,128]{1,0:T(8,128)} custom-call(s32[40960]{0:T(1024)} %broadcast_and_fusion.refs_0_, s32[33]{0:T(128)} %pad_add_fusion.1.refs_1_, f32[163840]{0:T(1024)} %bitcast.79, f32[32768,128]{1,0:T(8,128)} %get-tuple-element.8.refs_3_, bf16[8,3,4,64,1024]{4,3,2,1,0:T(8,128)(2,1)} %bitcast.109), custom_call_target="tpu_custom_call" | custom-call | flops 12884901888 | bytes 63012864 | tf_op jit(solution)/shard_map/moe_0/pallas_call | solution.py:283
  116.5 54.9 %all-gather.29.cloned.1.call-done = bf16[24,6,64,1024]{3,2,1,0:T(8,128)(2,1)} async-done(((bf16[3,6,64,1024]{3,2,1,0:T(8,128)(2,1)}), bf16[24,6,64,1024]{3,2,1,0:T(8,128)(2,1)}) %all-gather.29.cloned.1.call-update) | async-done | bytes 18874384 | tf_op jit(solution)/shard_map/all_gather | solution.py:324
  171.4 59.5 %moe_4.1.refs_5_ = f32[32832,128]{1,0:T(8,128)} custom-call(s32[40960]{0:T(1024)} %broadcast_and_fusion.refs_0_, s32[33]{0:T(128)} %pad_add_fusion.1.refs_1_, f32[163840]{0:T(1024)} %bitcast.80, f32[32768,128]{1,0:T(8,128)} %get-tuple-element.8.refs_3_, bf16[8,3,6,64,1024]{4,3,2,1,0:T(8,128)(2,1)} %bitcast.106, ...), custom_call_target="tpu_custom_call", output_to_operand_aliasing={{}: (5, {})} | custom-call | flops 19327352832 | bytes 69304320 | tf_op jit(solution)/shard_map/moe_4/pallas_call | solution.py:283
  230.9 32.7 %all-gather.27.cloned.1.call-done = bf16[24,6,64,1024]{3,2,1,0:T(8,128)(2,1)} async-done(((bf16[3,6,64,1024]{3,2,1,0:T(8,128)(2,1)}), bf16[24,6,64,1024]{3,2,1,0:T(8,128)(2,1)}) %all-gather.27.cloned.1.call-update) | async-done | bytes 18874384 | tf_op jit(solution)/shard_map/all_gather | solution.py:324
  263.6 48.6 %moe_10.1.refs_5_ = f32[32832,128]{1,0:T(8,128)} custom-call(s32[40960]{0:T(1024)} %broadcast_and_fusion.refs_0_, s32[33]{0:T(128)} %pad_add_fusion.1.refs_1_, f32[163840]{0:T(1024)} %bitcast.81, f32[32768,128]{1,0:T(8,128)} %get-tuple-element.8.refs_3_, bf16[8,3,6,64,1024]{4,3,2,1,0:T(8,128)(2,1)} %bitcast.107, ...), custom_call_target="tpu_custom_call", output_to_operand_aliasing={{}: (5, {})} | custom-call | flops 19327352832 | bytes 69304320 | tf_op jit(solution)/shard_map/moe_10/pallas_call | solution.py:283
  312.2 43.5 %all-gather.25.cloned.1.call-done = bf16[24,6,64,1024]{3,2,1,0:T(8,128)(2,1)} async-done(((bf16[3,6,64,1024]{3,2,1,0:T(8,128)(2,1)}), bf16[24,6,64,1024]{3,2,1,0:T(8,128)(2,1)}) %all-gather.25.cloned.1.call-update) | async-done | bytes 18874384 | tf_op jit(solution)/shard_map/all_gather | solution.py:324
  355.7 66.8 %moe_16.1.refs_5_ = f32[32832,128]{1,0:T(8,128)} custom-call(s32[40960]{0:T(1024)} %broadcast_and_fusion.refs_0_, s32[33]{0:T(128)} %pad_add_fusion.1.refs_1_, f32[163840]{0:T(1024)} %bitcast.82, f32[32768,128]{1,0:T(8,128)} %get-tuple-element.8.refs_3_, bf16[8,3,6,64,1024]{4,3,2,1,0:T(8,128)(2,1)} %bitcast.108, ...), custom_call_target="tpu_custom_call", output_to_operand_aliasing={{}: (5, {})} | custom-call | flops 19327352832 | bytes 69304320 | tf_op jit(solution)/shard_map/moe_16/pallas_call | solution.py:283
  422.5 34.1 %moe_22.1.refs_5_ = f32[32832,128]{1,0:T(8,128)} custom-call(s32[40960]{0:T(1024)} %broadcast_and_fusion.refs_0_, s32[33]{0:T(128)} %pad_add_fusion.1.refs_1_, f32[163840]{0:T(1024)} %bitcast.83, f32[32768,128]{1,0:T(8,128)} %get-tuple-element.8.refs_3_, bf16[8,3,4,64,1024]{4,3,2,1,0:T(8,128)(2,1)} %bitcast.78, ...), custom_call_target="tpu_custom_call", output_to_operand_aliasing={{}: (5, {})} | custom-call | flops 12884901888 | bytes 63012864 | tf_op jit(solution)/shard_map/moe_22/pallas_call | solution.py:283
  456.7 16.1 %all-gather.21.cloned.1.call-done = bf16[24,3,64,1024]{3,2,1,0:T(8,128)(2,1)} async-done(((bf16[3,3,64,1024]{3,2,1,0:T(8,128)(2,1)}), bf16[24,3,64,1024]{3,2,1,0:T(8,128)(2,1)}) %all-gather.21.cloned.1.call-update) | async-done | bytes 9437200 | tf_op jit(solution)/shard_map/all_gather | solution.py:324
  472.8 36.5 %moe_26.1.refs_5_ = f32[32832,128]{1,0:T(8,128)} custom-call(s32[40960]{0:T(1024)} %broadcast_and_fusion.refs_0_, s32[33]{0:T(128)} %pad_add_fusion.1.refs_1_, f32[163840]{0:T(1024)} %bitcast.84, f32[32768,128]{1,0:T(8,128)} %get-tuple-element.8.refs_3_, bf16[8,3,3,64,1024]{4,3,2,1,0:T(8,128)(2,1)} %bitcast.87, ...), custom_call_target="tpu_custom_call", output_to_operand_aliasing={{}: (5, {})} | custom-call | flops 9663676416 | bytes 59867136 | tf_op jit(solution)/shard_map/moe_26/pallas_call | solution.py:283
  509.2 1.9 all-gather.19.cloned.1.call-done
  511.1 33.4 %moe_29.1.refs_5_ = f32[32832,128]{1,0:T(8,128)} custom-call(s32[40960]{0:T(1024)} %broadcast_and_fusion.refs_0_, s32[33]{0:T(128)} %pad_add_fusion.1.refs_1_, f32[163840]{0:T(1024)} %bitcast.85, f32[32768,128]{1,0:T(8,128)} %get-tuple-element.8.refs_3_, bf16[8,3,2,64,1024]{4,3,2,1,0:T(8,128)(2,1)} %bitcast.88, ...), custom_call_target="tpu_custom_call", output_to_operand_aliasing={{}: (5, {})} | custom-call | flops 6442450944 | bytes 56721408 | tf_op jit(solution)/shard_map/moe_29/pallas_call | solution.py:283
  544.6 31.2 %moe_31.1 = bf16[4096,1024]{1,0:T(8,128)(2,1)} custom-call(s32[40960]{0:T(1024)} %broadcast_and_fusion.refs_0_, s32[33]{0:T(128)} %pad_add_fusion.1.refs_1_, f32[163840]{0:T(1024)} %bitcast.86, f32[32768,128]{1,0:T(8,128)} %get-tuple-element.8.refs_3_, bf16[8,3,1,64,1024]{4,3,2,1,0:T(8,128)(2,1)} %bitcast.99, f32[32832,128]{1,0:T(8,128)} %moe_29.1.refs_5_, ...), custom_call_target="tpu_custom_call" | custom-call | flops 3221225472 | bytes 53575680 | tf_op jit(solution)/shard_map/moe_31/pallas_call | solution.py:283
  (49 shorter events, 14.8 us)
Async XLA Ops:
  6.5 72.9 %all-gather.31.cloned.1.call-start = ((), (), s32[]{:S(2)}) async-start(), calls=%async_computation.7 | async-start | bytes 14155776 | tf_op jit(solution)/shard_map/all_gather | solution.py:324
  12.7 158.7 %all-gather.29.cloned.1.call-start = ((), (), s32[]{:S(2)}) async-start(), calls=%async_computation.6 | async-start | bytes 21233664 | tf_op jit(solution)/shard_map/all_gather | solution.py:324
  12.8 2.9 copy-start
  20.7 242.9 %all-gather.27.cloned.1.call-start = ((), (), s32[]{:S(2)}) async-start(), calls=%async_computation.5 | async-start | bytes 21233664 | tf_op jit(solution)/shard_map/all_gather | solution.py:324
  23.9 1.9 copy-start.1
  23.9 1.9 copy-start.2
  23.9 331.8 %all-gather.25.cloned.1.call-start = ((), (), s32[]{:S(2)}) async-start(), calls=%async_computation.4 | async-start | bytes 21233664 | tf_op jit(solution)/shard_map/all_gather | solution.py:324
  25.7 396.8 %all-gather.23.cloned.1.call-start = ((), (), s32[]{:S(2)}) async-start(), calls=%async_computation.3 | async-start | bytes 14155776 | tf_op jit(solution)/shard_map/all_gather | solution.py:324
  28.3 444.5 %all-gather.21.cloned.1.call-start = ((), (), s32[]{:S(2)}) async-start(), calls=%async_computation.2 | async-start | bytes 10616832 | tf_op jit(solution)/shard_map/all_gather | solution.py:324
  30.6 7.5 %copy-start.3 = (s32[4096,8]{0,1:T(8,128)S(1)}, s32[4096,8]{0,1:T(8,128)}, u32[]{:S(2)}) copy-start(s32[4096,8]{0,1:T(8,128)} %param.9) | copy-start | bytes 393220
  31.8 479.3 %all-gather.19.cloned.1.call-start = ((), (), s32[]{:S(2)}) async-start(), calls=%async_computation.1 | async-start | bytes 7077888 | tf_op jit(solution)/shard_map/all_gather | solution.py:324
  35.0 509.6 %all-gather.17.cloned.1.call-start = ((), (), s32[]{:S(2)}) async-start(), calls=%async_computation | async-start | bytes 3538944 | tf_op jit(solution)/shard_map/all_gather | solution.py:324
Sparse Core Ops, SparseCore 0:
  12.8 66.5 all-gather.30
  81.0 90.3 all-gather.28
  173.0 90.5 all-gather.26
  265.1 90.6 all-gather.24
  357.1 63.8 all-gather.22
  422.5 50.2 all-gather.20
  474.3 36.7 all-gather.18
  512.7 23.5 all-gather.16
